TPU v7x, 128 devices: a whole 4x4x4 slice. The times are simulated.
128 devices in a mesh: terms: 128 (over z, y, x, core).
Axes of the slice: x: 4, y: 4, z: 4, core: 2. Of those that a mesh axis runs over, the one named last changes fastest.
Arguments:
- psi: float32 [3, 128, 4, 4, 128], replicated
- left_env: bfloat16 [3072, 128, 128], P('terms')
- phys_op: bfloat16 [3072, 16, 16], P('terms')
- right_env: bfloat16 [3072, 128, 128], P('terms')
Outputs:
- output 1: float32 [3, 7, 128, 4, 4, 128], P(None, None, 'terms')
- output 2: float32 [3, 6], replicated
- output 3: float32 [3, 6], replicated
All inputs are finite; a program needn't handle non-finite values.
Results may differ from a plain program's by a relative error of at most 0.0113775.
Values are sent between devices in bfloat16 or wider.
A program may use at most 1 GiB of HBM per device.

v0:
```python
import jax
import jax.numpy as jnp
from jax import lax
from jax.sharding import PartitionSpec as P

LANCZOS_STEPS = 6


def solution(mesh):
    dev_count = mesh.shape['terms']

    def device_fn(psi, left_loc, phys_loc, right_loc):
        roots, bond_dim, phys_dim = psi.shape[0], psi.shape[1], psi.shape[2]
        pairs = phys_dim * phys_dim
        rows = bond_dim // dev_count
        n_elems = bond_dim * pairs * bond_dim
        psi_mat = psi.reshape(roots, bond_dim, pairs, bond_dim)
        norms = jnp.sqrt(jnp.sum(psi_mat * psi_mat, axis=(1, 2, 3)) / n_elems)
        v_full = psi_mat / norms[:, None, None, None]
        row_start = lax.axis_index('terms') * rows
        v_cur = lax.dynamic_slice_in_dim(v_full, row_start, rows, axis=1)
        v_in = v_full.astype(jnp.bfloat16)
        v_prev = jnp.zeros_like(v_cur)
        beta_prev = jnp.zeros((roots,), jnp.float32)
        vectors = [v_cur]
        alphas = []
        betas = []
        for step_idx in range(LANCZOS_STEPS):
            right_part = jnp.einsum('rcup,kbp->krcub', v_in, right_loc, preferred_element_type=jnp.float32).astype(jnp.bfloat16)
            mid_part = jnp.einsum('kqu,krcub->krcqb', phys_loc, right_part, preferred_element_type=jnp.float32).astype(jnp.bfloat16)
            part_sigma = jnp.einsum('kac,krcqb->raqb', left_loc, mid_part, preferred_element_type=jnp.float32)
            sigma = lax.psum_scatter(part_sigma, 'terms', scatter_dimension=1, tiled=True)
            alpha = lax.psum(jnp.sum(sigma * v_cur, axis=(1, 2, 3)), 'terms') / n_elems
            residual = sigma - alpha[:, None, None, None] * v_cur - beta_prev[:, None, None, None] * v_prev
            beta = jnp.sqrt(lax.psum(jnp.sum(residual * residual, axis=(1, 2, 3)), 'terms') / n_elems)
            v_next = residual / beta[:, None, None, None]
            if step_idx + 1 < LANCZOS_STEPS:
                v_in = lax.all_gather(v_next.astype(jnp.bfloat16), 'terms', axis=1, tiled=True)
            vectors.append(v_next)
            alphas.append(alpha)
            betas.append(beta)
            v_prev, v_cur, beta_prev = v_cur, v_next, beta
        stacked = jnp.stack(vectors, axis=1).reshape(roots, LANCZOS_STEPS + 1, rows, phys_dim, phys_dim, bond_dim)
        return stacked, jnp.stack(alphas, axis=1), jnp.stack(betas, axis=1)

    return jax.shard_map(device_fn, mesh=mesh, in_specs=(P(), P('terms'), P('terms'), P('terms')), out_specs=(P(None, None, 'terms'), P(), P()), check_vma=False)
```

profile of v0, /device:TPU:1, one launch (start us, length us, event | category | flops | bytes accessed | tf_op | source)
XLA Modules:
  0.0 2879.2 jit_solution(8199770353421440505)
XLA Ops:
  34.9 35.7 %convert_bitcast_fusion.10 = bf16[24,3,128,16,128]{4,3,2,1,0:T(8,128)(2,1)} fusion(bf16[24,16,16,1,1]{2,1,4,3,0:T(8,128)(2,1)S(1)} %copy.56, bf16[24,3,128,16,128]{4,2,0,3,1:T(8,128)(2,1)} %convert_bitcast_fusion.11), kind=kOutput, calls=%fused_computation.34 | convolution fusion | flops 622854144 | bytes 75509760 | tf_op jit(solution)/shard_map/kqu,krcub->krcqb/dot_general | solution.py:30
  104.8 211.7 %reduce-scatter.7.cloned.1.call-done = f32[3,1,16,128]{3,2,0,1:T(8,128)} async-done(((f32[3,128,16,128]{3,2,0,1:T(8,128)}), f32[3,1,16,128]{3,2,0,1:T(8,128)}) %reduce-scatter.7.cloned.1.call-update) | async-done | bytes 24592 | tf_op jit(solution)/shard_map/reduce_scatter | solution.py:32
  317.3 64.6 %psum.84 = f32[3]{0:T(128)S(1)} all-reduce(f32[3]{0:T(128)S(1)} %get-tuple-element.32), channel_id=1, replica_groups=mesh['terms'=128] {'terms'}, use_global_device_ids=true, to_apply=%region_3.0 | all-reduce | flops 3 | bytes 24 | tf_op jit(solution)/shard_map/psum | solution.py:33
  383.4 62.4 %psum.85 = f32[3]{0:T(128)S(1)} all-reduce(f32[3]{0:T(128)S(1)} %multiply_reduce_fusion.11), channel_id=1, replica_groups=mesh['terms'=128] {'terms'}, use_global_device_ids=true, to_apply=%region_5.0 | all-reduce | flops 3 | bytes 24 | tf_op jit(solution)/shard_map/psum | solution.py:35
  447.8 61.7 %all-gather.6.cloned.1.call-done = bf16[3,128,16,128]{3,2,0,1:T(8,128)(2,1)} async-done(((bf16[3,1,16,128]{3,2,0,1:T(8,128)(2,1)}), bf16[3,128,16,128]{3,2,0,1:T(8,128)(2,1)}) %all-gather.6.cloned.1.call-update) | async-done | bytes 1572880 | tf_op jit(solution)/shard_map/all_gather | solution.py:38
  596.9 205.5 %reduce-scatter.9.cloned.1.call-done = f32[3,1,16,128]{3,2,0,1:T(8,128)} async-done(((f32[3,128,16,128]{3,2,0,1:T(8,128)}), f32[3,1,16,128]{3,2,0,1:T(8,128)}) %reduce-scatter.9.cloned.1.call-update) | async-done | bytes 24592 | tf_op jit(solution)/shard_map/reduce_scatter | solution.py:32
  803.2 64.6 %psum.86 = f32[3]{0:T(128)S(1)} all-reduce(f32[3]{0:T(128)S(1)} %multiply_reduce_fusion.10), channel_id=1, replica_groups=mesh['terms'=128] {'terms'}, use_global_device_ids=true, to_apply=%region_8.0 | all-reduce | flops 3 | bytes 24 | tf_op jit(solution)/shard_map/psum | solution.py:33
  869.2 62.4 %psum.87 = f32[3]{0:T(128)S(1)} all-reduce(f32[3]{0:T(128)S(1)} %get-tuple-element.28), channel_id=1, replica_groups=mesh['terms'=128] {'terms'}, use_global_device_ids=true, to_apply=%region_10.0 | all-reduce | flops 3 | bytes 24 | tf_op jit(solution)/shard_map/psum | solution.py:35
  933.0 61.7 %all-gather.8.cloned.1.call-done = bf16[3,128,16,128]{3,2,0,1:T(8,128)(2,1)} async-done(((bf16[3,1,16,128]{3,2,0,1:T(8,128)(2,1)}), bf16[3,128,16,128]{3,2,0,1:T(8,128)(2,1)}) %all-gather.8.cloned.1.call-update) | async-done | bytes 1572880 | tf_op jit(solution)/shard_map/all_gather | solution.py:38
  1082.2 205.5 %reduce-scatter.11.cloned.1.call-done = f32[3,1,16,128]{3,2,0,1:T(8,128)} async-done(((f32[3,128,16,128]{3,2,0,1:T(8,128)}), f32[3,1,16,128]{3,2,0,1:T(8,128)}) %reduce-scatter.11.cloned.1.call-update) | async-done | bytes 24592 | tf_op jit(solution)/shard_map/reduce_scatter | solution.py:32
  1288.5 64.6 %psum.88 = f32[3]{0:T(128)S(1)} all-reduce(f32[3]{0:T(128)S(1)} %multiply_reduce_fusion.8), channel_id=1, replica_groups=mesh['terms'=128] {'terms'}, use_global_device_ids=true, to_apply=%region_13.0 | all-reduce | flops 3 | bytes 24 | tf_op jit(solution)/shard_map/psum | solution.py:33
  1354.6 62.4 %psum.89 = f32[3]{0:T(128)S(1)} all-reduce(f32[3]{0:T(128)S(1)} %get-tuple-element.24), channel_id=1, replica_groups=mesh['terms'=128] {'terms'}, use_global_device_ids=true, to_apply=%region_15.0 | all-reduce | flops 3 | bytes 24 | tf_op jit(solution)/shard_map/psum | solution.py:35
  1418.4 61.7 %all-gather.10.cloned.1.call-done = bf16[3,128,16,128]{3,2,0,1:T(8,128)(2,1)} async-done(((bf16[3,1,16,128]{3,2,0,1:T(8,128)(2,1)}), bf16[3,128,16,128]{3,2,0,1:T(8,128)(2,1)}) %all-gather.10.cloned.1.call-update) | async-done | bytes 1572880 | tf_op jit(solution)/shard_map/all_gather | solution.py:38
  1567.4 205.5 %reduce-scatter.13.cloned.1.call-done = f32[3,1,16,128]{3,2,0,1:T(8,128)} async-done(((f32[3,128,16,128]{3,2,0,1:T(8,128)}), f32[3,1,16,128]{3,2,0,1:T(8,128)}) %reduce-scatter.13.cloned.1.call-update) | async-done | bytes 24592 | tf_op jit(solution)/shard_map/reduce_scatter | solution.py:32
  1773.7 64.6 %psum.90 = f32[3]{0:T(128)S(1)} all-reduce(f32[3]{0:T(128)S(1)} %multiply_reduce_fusion.6), channel_id=1, replica_groups=mesh['terms'=128] {'terms'}, use_global_device_ids=true, to_apply=%region_18.0 | all-reduce | flops 3 | bytes 24 | tf_op jit(solution)/shard_map/psum | solution.py:33
  1839.2 62.4 %psum.91 = f32[3]{0:T(128)S(1)} all-reduce(f32[3]{0:T(128)S(1)} %get-tuple-element.20), channel_id=1, replica_groups=mesh['terms'=128] {'terms'}, use_global_device_ids=true, to_apply=%region_20.0 | all-reduce | flops 3 | bytes 24 | tf_op jit(solution)/shard_map/psum | solution.py:35
  1902.4 61.7 %all-gather.12.cloned.1.call-done = bf16[3,128,16,128]{3,2,0,1:T(8,128)(2,1)} async-done(((bf16[3,1,16,128]{3,2,0,1:T(8,128)(2,1)}), bf16[3,128,16,128]{3,2,0,1:T(8,128)(2,1)}) %all-gather.12.cloned.1.call-update) | async-done | bytes 1572880 | tf_op jit(solution)/shard_map/all_gather | solution.py:38
  2051.6 205.5 %reduce-scatter.15.cloned.1.call-done = f32[3,1,16,128]{3,2,0,1:T(8,128)} async-done(((f32[3,128,16,128]{3,2,0,1:T(8,128)}), f32[3,1,16,128]{3,2,0,1:T(8,128)}) %reduce-scatter.15.cloned.1.call-update) | async-done | bytes 24592 | tf_op jit(solution)/shard_map/reduce_scatter | solution.py:32
  2258.0 64.6 %psum.92 = f32[3]{0:T(128)S(1)} all-reduce(f32[3]{0:T(128)S(1)} %multiply_reduce_fusion.4), channel_id=1, replica_groups=mesh['terms'=128] {'terms'}, use_global_device_ids=true, to_apply=%region_23.0 | all-reduce | flops 3 | bytes 24 | tf_op jit(solution)/shard_map/psum | solution.py:33
  2323.4 62.4 %psum.93 = f32[3]{0:T(128)S(1)} all-reduce(f32[3]{0:T(128)S(1)} %get-tuple-element.16), channel_id=1, replica_groups=mesh['terms'=128] {'terms'}, use_global_device_ids=true, to_apply=%region_25.0 | all-reduce | flops 3 | bytes 24 | tf_op jit(solution)/shard_map/psum | solution.py:35
  2386.6 61.7 %all-gather.14.cloned.1.call-done = bf16[3,128,16,128]{3,2,0,1:T(8,128)(2,1)} async-done(((bf16[3,1,16,128]{3,2,0,1:T(8,128)(2,1)}), bf16[3,128,16,128]{3,2,0,1:T(8,128)(2,1)}) %all-gather.14.cloned.1.call-update) | async-done | bytes 1572880 | tf_op jit(solution)/shard_map/all_gather | solution.py:38
  2535.7 205.5 %reduce-scatter.17.cloned.1.call-done = f32[3,1,16,128]{3,2,0,1:T(8,128)} async-done(((f32[3,128,16,128]{3,2,0,1:T(8,128)}), f32[3,1,16,128]{3,2,0,1:T(8,128)}) %reduce-scatter.17.cloned.1.call-update) | async-done | bytes 24592 | tf_op jit(solution)/shard_map/reduce_scatter | solution.py:32
  2742.1 64.6 %psum.94 = f32[3]{0:T(128)S(1)} all-reduce(f32[3]{0:T(128)S(1)} %multiply_reduce_fusion.2), channel_id=1, replica_groups=mesh['terms'=128] {'terms'}, use_global_device_ids=true, to_apply=%region_28.0 | all-reduce | flops 3 | bytes 24 | tf_op jit(solution)/shard_map/psum | solution.py:33
  2807.6 62.4 %psum.95 = f32[3]{0:T(128)S(1)} all-reduce(f32[3]{0:T(128)S(1)} %get-tuple-element.12), channel_id=1, replica_groups=mesh['terms'=128] {'terms'}, use_global_device_ids=true, to_apply=%region_30.0 | all-reduce | flops 3 | bytes 24 | tf_op jit(solution)/shard_map/psum | solution.py:35
  (116 shorter events, 519.2 us)
Async XLA Ops:
  7.2 12.0 copy-start
  7.2 309.3 %reduce-scatter.7.cloned.1.call-start = ((), (), s32[]{:S(2)}) async-start(), calls=%async_computation.6 | async-start | bytes 3170304 | tf_op jit(solution)/shard_map/reduce_scatter | solution.py:32
  34.9 35.7 %copy-start.11 = (bf16[24,128,128]{2,1,0:T(8,128)(2,1)S(1)}, bf16[24,128,128]{2,1,0:T(8,128)(2,1)}, u32[]{:S(2)}) copy-start(bf16[24,128,128]{2,1,0:T(8,128)(2,1)} %param.5) | copy-start | bytes 2359300
  104.7 404.8 %all-gather.6.cloned.1.call-start = ((), (), s32[]{:S(2)}) async-start(), calls=%async_computation.7 | async-start | bytes 1585152 | tf_op jit(solution)/shard_map/all_gather | solution.py:38
  317.3 551.0 %copy-start.1 = (f32[3,1,16,128]{3,2,0,1:T(8,128)}, f32[3,1,16,128]{3,2,0,1:T(8,128)S(1)}, u32[]{:S(2)}) copy-start(f32[3,1,16,128]{3,2,0,1:T(8,128)S(1)} %get-tuple-element.33) | copy-start | bytes 73732
  447.8 905.9 %copy-start.3 = (f32[3,1,16,128]{3,2,0,1:T(8,128)}, f32[3,1,16,128]{3,2,0,1:T(8,128)S(1)}, u32[]{:S(2)}) copy-start(f32[3,1,16,128]{3,2,0,1:T(8,128)S(1)} %get-tuple-element.31) | copy-start | bytes 73732
  447.8 354.6 %reduce-scatter.9.cloned.1.call-start = ((), (), s32[]{:S(2)}) async-start(), calls=%async_computation.8 | async-start | bytes 3170304 | tf_op jit(solution)/shard_map/reduce_scatter | solution.py:32
  596.8 397.9 %all-gather.8.cloned.1.call-start = ((), (), s32[]{:S(2)}) async-start(), calls=%async_computation.9 | async-start | bytes 1585152 | tf_op jit(solution)/shard_map/all_gather | solution.py:38
  932.9 354.7 %reduce-scatter.11.cloned.1.call-start = ((), (), s32[]{:S(2)}) async-start(), calls=%async_computation.10 | async-start | bytes 3170304 | tf_op jit(solution)/shard_map/reduce_scatter | solution.py:32
  1082.1 397.9 %all-gather.10.cloned.1.call-start = ((), (), s32[]{:S(2)}) async-start(), calls=%async_computation.11 | async-start | bytes 1585152 | tf_op jit(solution)/shard_map/all_gather | solution.py:38
  1418.3 354.6 %reduce-scatter.13.cloned.1.call-start = ((), (), s32[]{:S(2)}) async-start(), calls=%async_computation.12 | async-start | bytes 3170304 | tf_op jit(solution)/shard_map/reduce_scatter | solution.py:32
  1567.3 396.8 %all-gather.12.cloned.1.call-start = ((), (), s32[]{:S(2)}) async-start(), calls=%async_computation.13 | async-start | bytes 1585152 | tf_op jit(solution)/shard_map/all_gather | solution.py:38
  1902.4 354.7 %reduce-scatter.15.cloned.1.call-start = ((), (), s32[]{:S(2)}) async-start(), calls=%async_computation.14 | async-start | bytes 3170304 | tf_op jit(solution)/shard_map/reduce_scatter | solution.py:32
  2051.5 396.8 %all-gather.14.cloned.1.call-start = ((), (), s32[]{:S(2)}) async-start(), calls=%async_computation.15 | async-start | bytes 1585152 | tf_op jit(solution)/shard_map/all_gather | solution.py:38
  2386.6 354.6 %reduce-scatter.17.cloned.1.call-start = ((), (), s32[]{:S(2)}) async-start(), calls=%async_computation.16 | async-start | bytes 3170304 | tf_op jit(solution)/shard_map/reduce_scatter | solution.py:32
  2501.4 34.2 %copy-start.2 = (f32[3,1,16,128]{3,2,0,1:T(8,128)S(1)}, f32[3,1,16,128]{3,2,0,1:T(8,128)}, u32[]{:S(2)}) copy-start(f32[3,1,16,128]{3,2,0,1:T(8,128)} %copy-done.1) | copy-start | bytes 73732
  2501.4 34.2 %copy-start.4 = (f32[3,1,16,128]{3,2,0,1:T(8,128)S(1)}, f32[3,1,16,128]{3,2,0,1:T(8,128)}, u32[]{:S(2)}) copy-start(f32[3,1,16,128]{3,2,0,1:T(8,128)} %copy-done.3) | copy-start | bytes 73732
  2501.5 368.6 %copy-start.6 = (f32[3,1]{0,1:T(1,128)S(1)}, f32[3,1]{0,1:T(1,128)}, u32[]{:S(2)}) copy-start(f32[3,1]{0,1:T(1,128)} %get-tuple-element.46) | copy-start | bytes 40
  2501.5 368.6 %copy-start.8 = (f32[3,1]{0,1:T(1,128)S(1)}, f32[3,1]{0,1:T(1,128)}, u32[]{:S(2)}) copy-start(f32[3,1]{0,1:T(1,128)} %get-tuple-element.44) | copy-start | bytes 40
  2501.5 368.6 %copy-start.10 = (f32[3,1]{0,1:T(1,128)S(1)}, f32[3,1]{0,1:T(1,128)}, u32[]{:S(2)}) copy-start(f32[3,1]{0,1:T(1,128)} %get-tuple-element.42) | copy-start | bytes 40
  2501.5 369.3 %copy-start.5 = (f32[3,1]{0,1:T(1,128)S(1)}, f32[3,1]{0,1:T(1,128)}, u32[]{:S(2)}) copy-start(f32[3,1]{0,1:T(1,128)} %get-tuple-element.58) | copy-start | bytes 40
  2501.5 369.3 %copy-start.7 = (f32[3,1]{0,1:T(1,128)S(1)}, f32[3,1]{0,1:T(1,128)}, u32[]{:S(2)}) copy-start(f32[3,1]{0,1:T(1,128)} %get-tuple-element.56) | copy-start | bytes 40
  2501.5 369.3 %copy-start.9 = (f32[3,1]{0,1:T(1,128)S(1)}, f32[3,1]{0,1:T(1,128)}, u32[]{:S(2)}) copy-start(f32[3,1]{0,1:T(1,128)} %get-tuple-element.54) | copy-start | bytes 40
Sparse Core Ops, SparseCore 0:
  104.8 211.5 reduce-scatter.6
  447.9 61.5 all-gather.5
  596.9 205.4 reduce-scatter.8
  933.0 61.5 all-gather.7
  1082.2 205.3 reduce-scatter.10
  1418.4 61.5 all-gather.9
  1567.4 205.3 reduce-scatter.12
  1902.5 61.5 all-gather.11
  2051.7 205.3 reduce-scatter.14
  2386.7 61.5 all-gather.13
  2535.8 205.4 reduce-scatter.16
where the time goes:
time: 2890 us; the launch traced here: 2880 us
  waiting for transfers between devices  1550 us (54%)
  blocking collectives  762 us (26%)
  matrix products  500 us (17%)
    reduce_scatter x6, waiting for transfers between devices, device_fn(): lax.psum_scatter(part_sigma, 'terms', scatter_dimension=1, tiled=True)  1240 us
    psum x6, blocking collectives, device_fn(): alpha = lax.psum(jnp.sum(sigma * v_cur, axis=(1, 2, 3)), 'terms') / n_elems  388 us
    psum x6, blocking collectives, device_fn(): lax.psum(jnp.sum(residual * residual, axis=(1, 2, 3)), 'terms') / n_elems  375 us
    all_gather x5, waiting for transfers between devices, device_fn(): lax.all_gather(v_next.astype(jnp.bfloat16), 'terms', axis=1, tiled=True)  308 us
    dot_general x6, matrix products, device_fn(): jnp.einsum('kqu,krcub->krcqb', phys_loc, right_part, preferred_element_ty...  213 us
    dot_general x6, matrix products, device_fn(): jnp.einsum('kac,krcqb->raqb', left_loc, mid_part, preferred_element_type=...  183 us
    dot_general x6, matrix products, device_fn(): jnp.einsum('rcup,kbp->krcub', v_in, right_loc, preferred_element_type=jnp...  104 us
  transfers between devices with their start and end apart: 11, of which 11 were waited for; matrix products, arithmetic and copies ran while one was open for 0% of the time, Pallas kernels for 0%

commit v1 on v0

v1 whole, which is shorter than its diff:
```python
import functools

import jax
import jax.numpy as jnp
from jax import lax
from jax.experimental import pallas as pl
from jax.experimental.pallas import tpu as pltpu
from jax.sharding import PartitionSpec as P

LANCZOS_STEPS = 6
MESH = pl.DeviceIdType.MESH
F32 = jnp.float32
BF16 = jnp.bfloat16
ITERS = 6


def lanczos_kernel(topo, steps, psi_ref, left_ref, phys_ref, right_ref, vec_ref, alpha_ref, beta_ref,
                   v, u, wide, za, zb, acc, wbuf, rc, rx, ry, rz, beta_prev, send_sem, recv_sem):
    nz, ny, nx, nc = topo
    roots, rows = psi_ref.shape[0], psi_ref.shape[1]
    bond = psi_ref.shape[2]
    pairs = rows // bond
    n_elems = rows * bond
    terms = left_ref.shape[0]
    me = lax.axis_index('terms')
    c = lax.rem(me, nc)
    x = lax.rem(me // nc, nx)
    y = lax.rem(me // (nc * nx), ny)
    z = me // (nc * nx * ny)
    rows_c, rows_x = rows // nc, rows // (nc * nx)
    rows_y, rows_z = rows // (nc * nx * ny), rows // (nc * nx * ny * nz)
    base_c = c * rows_c
    base_x = base_c + x * rows_x
    base_y = base_x + y * rows_y
    base_z = base_y + z * rows_z

    def device(zz, yy, xx, cc):
        return ((zz * ny + yy) * nx + xx) * nc + cc

    def hop(axis, d):
        if axis == 'c':
            cc = lax.rem(c + d, nc)
            return device(z, y, x, cc), cc
        if axis == 'x':
            xx = lax.rem(x + d, nx)
            return device(z, y, xx, c), xx
        if axis == 'y':
            yy = lax.rem(y + d, ny)
            return device(z, yy, x, c), yy
        zz = lax.rem(z + d, nz)
        return device(zz, y, x, c), zz

    sizes = {'c': nc, 'x': nx, 'y': ny, 'z': nz}
    scatter = {'c': (0, 0, rows_c, rc, 0), 'x': (base_c, 1, rows_x, rx, 1), 'y': (base_x, 2, rows_y, ry, 4),
               'z': (base_y, 3, rows_z, rz, 7)}
    gather = {'z': (base_z, rows_z, 10), 'y': (base_y, rows_y, 13), 'x': (base_x, rows_x, 16), 'c': (base_c, rows_c, 19)}

    def scatter_copies(r, axis):
        start, _, count, buf, sem0 = scatter[axis]
        out = []
        for d in range(1, sizes[axis]):
            dev, coord = hop(axis, d)
            out.append(pltpu.make_async_remote_copy(
                src_ref=acc.at[r, pl.ds(pl.multiple_of(start + coord * count, 8), count)],
                dst_ref=buf.at[r, d - 1],
                send_sem=send_sem.at[r, sem0 + d - 1], recv_sem=recv_sem.at[r, sem0 + d - 1],
                device_id=(dev,), device_id_type=MESH))
        return out

    def gather_copies(r, axis):
        start, count, sem0 = gather[axis]
        out = []
        for d in range(1, sizes[axis]):
            dev, _ = hop(axis, d)
            block = wbuf.at[r, pl.ds(pl.multiple_of(start, 8), count)]
            out.append(pltpu.make_async_remote_copy(
                src_ref=block, dst_ref=block,
                send_sem=send_sem.at[r, sem0 + d - 1], recv_sem=recv_sem.at[r, sem0 + d - 1],
                device_id=(dev,), device_id_type=MESH))
        return out

    def start(copies):
        for copy in copies:
            copy.start()

    def wait(copies):
        for copy in copies:
            copy.wait_send()
        for copy in copies:
            copy.wait_recv()

    own = {'c': base_c, 'x': base_x, 'y': base_y, 'z': base_z}

    def reduce_own(r, axis):
        _, _, count, buf, _ = scatter[axis]
        chunk = min(count, 128)

        def body(i, carry):
            at = pl.ds(pl.multiple_of(own[axis] + i * chunk, 8), chunk)
            inside = pl.ds(pl.multiple_of(i * chunk, 8), chunk)
            total = acc[r, at, :]
            for d in range(sizes[axis] - 1):
                total = total + buf[r, d, inside, :]
            if axis == 'z':
                wbuf[r, at, :] = total
            else:
                acc[r, at, :] = total
            return carry

        lax.fori_loop(0, count // chunk, body, 0)

    barrier = pltpu.get_barrier_semaphore()
    peers = [hop(axis, d)[0] for axis in 'cxyz' for d in range(1, sizes[axis])]
    for dev in peers:
        pl.semaphore_signal(barrier, inc=1, device_id=(dev,), device_id_type=MESH)
    pl.semaphore_wait(barrier, len(peers))

    big = pairs * 16
    row = lax.broadcasted_iota(jnp.int32, (big, pairs), 0) // 16
    spread = jnp.where(row == lax.broadcasted_iota(jnp.int32, (big, pairs), 1), 1.0, 0.0).astype(BF16)
    col = lax.broadcasted_iota(jnp.int32, (pairs, big), 1) // 16
    spread_t = jnp.where(col == lax.broadcasted_iota(jnp.int32, (pairs, big), 0), 1.0, 0.0).astype(BF16)
    diagonal = (lax.rem(lax.broadcasted_iota(jnp.int32, (big, big), 0), 16)
                == lax.rem(lax.broadcasted_iota(jnp.int32, (big, big), 1), 16))

    def expand(k, carry):
        tall = jnp.dot(spread, phys_ref[k], preferred_element_type=F32).astype(BF16)
        full = jnp.dot(tall, spread_t, preferred_element_type=F32)
        wide[k] = jnp.where(diagonal, full, 0.0).astype(BF16)
        return carry

    lax.fori_loop(0, terms, expand, 0)

    chunk = 2 * bond
    chunks = rows // chunk

    def fold(t):
        return jnp.sum(t.reshape(chunk // 8, 8, bond), axis=0)

    def total(t):
        return jnp.sum(t, axis=(0, 1), keepdims=True)

    def put_vector(r, nxt, i, part):
        v[r, nxt, pl.ds(pl.multiple_of(i * chunk, 8), chunk), :] = part
        u[r, pl.ds(2 * i, 2)] = part.reshape(2, bond, bond).astype(BF16)

    def put_row(r, nxt, j):
        vec_ref[r, j] = v[r, nxt, pl.ds(me, pairs, stride=bond), :]

    def first_vector(r, carry):
        def norm_body(i, s):
            part = psi_ref[r, pl.ds(pl.multiple_of(i * chunk, 8), chunk), :]
            return s + fold(part * part)

        norm = jnp.sqrt(total(lax.fori_loop(0, chunks, norm_body, jnp.zeros((8, bond), F32))) / n_elems)

        def scale_body(i, s):
            at = pl.ds(pl.multiple_of(i * chunk, 8), chunk)
            put_vector(r, 0, i, psi_ref[r, at, :] / norm)
            v[r, 1, at, :] = jnp.zeros((chunk, bond), F32)
            return s

        lax.fori_loop(0, chunks, scale_body, 0)
        beta_prev[r] = jnp.zeros((8, bond), F32)
        put_row(r, 0, 0)
        return carry

    lax.fori_loop(0, roots, first_vector, 0)

    def update(r, j):
        cur, nxt = lax.rem(j, 2), lax.rem(j + 1, 2)
        rowsof = lambda i: pl.ds(pl.multiple_of(i * chunk, 8), chunk)

        def alpha_body(i, s):
            return s + fold(wbuf[r, rowsof(i), :] * v[r, cur, rowsof(i), :])

        alpha = total(lax.fori_loop(0, chunks, alpha_body, jnp.zeros((8, bond), F32))) / n_elems
        before = beta_prev[r][0:1, 0:1]

        def residual_body(i, s):
            at = rowsof(i)
            res = wbuf[r, at, :] - alpha * v[r, cur, at, :] - before * v[r, nxt, at, :]
            wbuf[r, at, :] = res
            return s + fold(res * res)

        beta = jnp.sqrt(total(lax.fori_loop(0, chunks, residual_body, jnp.zeros((8, bond), F32))) / n_elems)

        def next_body(i, s):
            put_vector(r, nxt, i, wbuf[r, rowsof(i), :] / beta)
            return s

        lax.fori_loop(0, chunks, next_body, 0)
        alpha_ref[r, j] = jnp.broadcast_to(alpha, (8, bond))
        beta_ref[r, j] = jnp.broadcast_to(beta, (8, bond))
        beta_prev[r] = jnp.broadcast_to(beta, (8, bond))
        put_row(r, nxt, j + 1)

    def right_mid(r, p, dst):
        rp = jnp.concatenate([right_ref[2 * p], right_ref[2 * p + 1]], axis=1)
        for g2 in range(bond // 32):
            ys = []
            for g in (2 * g2, 2 * g2 + 1):
                lhs = u[r, :, g * 16:(g + 1) * 16, :].reshape(big, bond)
                ys.append(jnp.dot(lhs, rp, preferred_element_type=F32).astype(BF16))
            for k in range(2):
                rhs = jnp.concatenate([t[:, k * bond:(k + 1) * bond] for t in ys], axis=1)
                out = jnp.dot(wide[2 * p + k], rhs, preferred_element_type=F32).astype(BF16)
                for h in range(2):
                    g = 2 * g2 + h
                    dst[k, :, g * 16:(g + 1) * 16, :] = out[:, h * bond:(h + 1) * bond].reshape(pairs, 16, bond)

    def left(r, p, first):
        lp = jnp.concatenate([left_ref[2 * p + k] for k in range(4)], axis=1)
        for qp in range(pairs // 2):
            cols = []
            for q in (2 * qp, 2 * qp + 1):
                cols.append(jnp.concatenate([za[0, q], za[1, q], zb[0, q], zb[1, q]], axis=0))
            out = jnp.dot(lp, jnp.concatenate(cols, axis=1), preferred_element_type=F32)
            for h in range(2):
                q = 2 * qp + h
                at = pl.ds(q * bond, bond)
                acc[r, at, :] += out[:, h * bond:(h + 1) * bond]

    per_iter = terms // ITERS

    slots = roots * steps

    def slot(s, carry):
        r = lax.rem(s, roots)
        r1 = lax.rem(s + roots - 1, roots)
        r2 = lax.rem(s + roots - 2, roots)
        computing = s < slots
        scattering = jnp.logical_and(s >= 1, s < slots + 1)
        gathering = s >= 2

        @pl.when(computing)
        def _():
            def clear(i, t):
                acc[r, pl.ds(pl.multiple_of(i * chunk, 8), chunk), :] = jnp.zeros((chunk, bond), F32)
                return t
            lax.fori_loop(0, chunks, clear, 0)

        def step(i, t):
            @pl.when(jnp.logical_and(gathering, i == 1))
            def _():
                wait(gather_copies(r2, 'z'))
                start(gather_copies(r2, 'y'))

            @pl.when(jnp.logical_and(gathering, i == 3))
            def _():
                wait(gather_copies(r2, 'y'))
                start(gather_copies(r2, 'x'))

            @pl.when(jnp.logical_and(scattering, i == 1))
            def _():
                wait(scatter_copies(r1, 'c'))
                reduce_own(r1, 'c')
                start(scatter_copies(r1, 'x'))

            @pl.when(jnp.logical_and(scattering, i == 4))
            def _():
                wait(scatter_copies(r1, 'x'))
                reduce_own(r1, 'x')
                start(scatter_copies(r1, 'y'))

            @pl.when(computing)
            def _():
                for m in range(per_iter // 4):
                    p = i * (per_iter // 2) + 2 * m
                    right_mid(r, p, za)
                    right_mid(r, p + 1, zb)
                    left(r, p, m == 0)
            return t

        lax.fori_loop(0, ITERS, step, 0)

        @pl.when(gathering)
        def _():
            wait(gather_copies(r2, 'x'))
            start(gather_copies(r2, 'c'))

        @pl.when(computing)
        def _():
            start(scatter_copies(r, 'c'))

        @pl.when(scattering)
        def _():
            wait(scatter_copies(r1, 'y'))
            reduce_own(r1, 'y')
            start(scatter_copies(r1, 'z'))

        @pl.when(gathering)
        def _():
            wait(gather_copies(r2, 'c'))
            update(r2, (s - 2) // roots)

        @pl.when(scattering)
        def _():
            wait(scatter_copies(r1, 'z'))
            reduce_own(r1, 'z')
            start(gather_copies(r1, 'z'))
        return carry

    lax.fori_loop(0, slots + 2, slot, 0)


def build(topo, steps, roots, bond, pairs, terms):
    nz, ny, nx, nc = topo
    rows = pairs * bond
    vm = pl.BlockSpec(memory_space=pltpu.VMEM)
    rows_c, rows_x = rows // nc, rows // (nc * nx)
    rows_y, rows_z = rows_x // ny, rows_x // (ny * nz)
    return pl.pallas_call(
        functools.partial(lanczos_kernel, topo, steps),
        out_shape=(jax.ShapeDtypeStruct((roots, steps + 1, pairs, bond), F32),
                   jax.ShapeDtypeStruct((roots, steps, 8, bond), F32),
                   jax.ShapeDtypeStruct((roots, steps, 8, bond), F32)),
        in_specs=[vm] * 4,
        out_specs=(vm, vm, vm),
        scratch_shapes=[
            pltpu.VMEM((roots, 2, rows, bond), F32),
            pltpu.VMEM((roots, pairs, bond, bond), BF16),
            pltpu.VMEM((terms, pairs * 16, pairs * 16), BF16),
            pltpu.VMEM((2, pairs, bond, bond), BF16),
            pltpu.VMEM((2, pairs, bond, bond), BF16),
            pltpu.VMEM((roots, rows, bond), F32),
            pltpu.VMEM((roots, rows, bond), F32),
            pltpu.VMEM((roots, nc - 1, rows_c, bond), F32),
            pltpu.VMEM((roots, nx - 1, rows_x, bond), F32),
            pltpu.VMEM((roots, ny - 1, rows_y, bond), F32),
            pltpu.VMEM((roots, nz - 1, rows_z, bond), F32),
            pltpu.VMEM((roots, 8, bond), F32),
            pltpu.SemaphoreType.DMA((roots, 20)),
            pltpu.SemaphoreType.DMA((roots, 20)),
        ],
        compiler_params=pltpu.CompilerParams(collective_id=0, has_side_effects=True,
                                             vmem_limit_bytes=60 * 1024 * 1024),
        name='lanczos',
    )


def solution(mesh, topo=(4, 4, 4, 2), steps=LANCZOS_STEPS):
    def device_fn(psi, left_loc, phys_loc, right_loc):
        roots, bond, phys = psi.shape[0], psi.shape[1], psi.shape[2]
        pairs = phys * phys
        psi_rows = psi.reshape(roots, bond, pairs, psi.shape[4]).transpose(0, 2, 1, 3).reshape(roots, pairs * bond, bond)
        vecs, alpha, beta = build(topo, steps, roots, bond, pairs, left_loc.shape[0])(psi_rows, left_loc, phys_loc, right_loc)
        return (vecs.reshape(roots, steps + 1, 1, phys, phys, bond), alpha[:, :, 0, 0], beta[:, :, 0, 0])

    return jax.shard_map(device_fn, mesh=mesh, in_specs=(P(), P('terms'), P('terms'), P('terms')),
                         out_specs=(P(None, None, 'terms'), P(), P()), check_vma=False)
```

time: 2890 us -> 438 us (0.15)
  waiting for transfers between devices: 1550 us -> 0 us
  blocking collectives: 762 us -> 0 us
  matrix products: 500 us -> 0 us
  Pallas kernels: 0 us -> 428 us
    reduce_scatter x6 -> x0, waiting for transfers between devices: 1240 us -> none  [device_fn(): lax.psum_scatter(part_sigma, 'terms', scatter_dimension=1, tiled=True)]
    psum x12 -> x0, blocking collectives: 762 us -> none  [the longest x6 388 us: device_fn(): alpha = lax.psum(jnp.sum(sigma * v_cur, axis=(1, 2, 3)), 'terms') / n_elems]
    dot_general x18 -> x0, matrix products: 500 us -> none  [the longest x6 213 us: device_fn(): jnp.einsum('kqu,krcub->krcqb', phys_loc, right_part, preferred_element_ty...]
    pallas_call x0 -> x1, Pallas kernels: none -> 428 us  [device_fn(): build(topo, steps, roots, bond, pairs, left_loc.shape[0])]
    all_gather x5 -> x0, waiting for transfers between devices: 308 us -> none  [device_fn(): lax.all_gather(v_next.astype(jnp.bfloat16), 'terms', axis=1, tiled=True)]
  transfers between devices with their start and end apart: 11 -> 0, of which waited for: 11 -> 0; matrix products, arithmetic and copies ran while one was open for 0% -> 0% of each run, Pallas kernels for 0% -> 0%
where the time goes in v1:
time: 438 us
  Pallas kernels  428 us (98%)
  local copies, waits for them, and re-layouts  9.35 us (2%)
    pallas_call x1, Pallas kernels, device_fn(): build(topo, steps, roots, bond, pairs, left_loc.shape[0])  428 us

profile of v1, /device:TPU:1, one launch (start us, length us, event | category | flops | bytes accessed | tf_op | source)
XLA Modules:
  0.0 437.8 jit_solution(7457604875917500004)
XLA Ops:
  0.6 1.6 copy.11.phys_ref
  2.2 4.5 %copy.10 = f32[3,128,16,128]{3,1,2,0:T(8,128)} copy(f32[3,128,16,128]{3,2,1,0:T(8,128)} %bitcast.8) | data formatting | bytes 6291456 | tf_op jit(solution)/shard_map/reshape | solution.py:346
  6.7 427.8 %lanczos.1 = (f32[3,7,16,128]{3,2,1,0:T(8,128)}, f32[3,6,8,128]{3,2,1,0:T(8,128)}, f32[3,6,8,128]{3,2,1,0:T(8,128)}) custom-call(f32[3,2048,128]{2,1,0:T(8,128)} %bitcast.7, bf16[24,128,128]{2,1,0:T(8,128)(2,1)} %left_ref.1, bf16[24,16,16]{2,1,0:T(8,128)(2,1)} %copy.11.phys_ref, bf16[24,128,128]{2,1,0:T(8,128)(2,1)} %right_ref.1), custom_call_target="tpu_custom_call" | custom-call | tf_op jit(solution)/shard_map/lanczos/pallas_call | solution.py:347
  434.5 1.6 slice_reduce_fusion
  436.2 1.6 copy.14

commit v2 on v0

v2 whole, which is shorter than its diff:
```python
import functools

import jax
import jax.numpy as jnp
from jax import lax
from jax.experimental import pallas as pl
from jax.experimental.pallas import tpu as pltpu
from jax.sharding import PartitionSpec as P

LANCZOS_STEPS = 6
MESH = pl.DeviceIdType.MESH
F32 = jnp.float32
BF16 = jnp.bfloat16
PAIRS_PER_ITER = 3
SCATTER_HOOK = 3
GATHER_HOOK = 2
SEMS = 19


def lanczos_kernel(topo, steps, psi_ref, left_ref, phys_ref, right_ref, vec_ref, alpha_ref, beta_ref,
                   v, u, wide, zbuf, acc, wbuf, rc, rr, rp, beta_prev, send_sem, recv_sem):
    n = topo
    roots, rows, bond = psi_ref.shape
    pairs = rows // bond
    n_elems = rows * bond
    terms = left_ref.shape[0]
    plane = n * n
    half = pairs // 2
    quarter = half // 2
    strip = bond // plane
    me = lax.axis_index('terms')
    c = lax.rem(me, 2)
    x = lax.rem(me // 2, n)
    y = lax.rem(me // (2 * n), n)
    z = me // (2 * n * n)

    def device(zz, yy, xx, cc):
        return ((zz * n + yy) * n + xx) * 2 + cc

    sibling = device(z, y, x, 1 - c)

    ring_at = (x, y)
    plane_at = (y * n + z, z * n + x)

    def ring_peer(p, d):
        if p == 0:
            coord = lax.rem(x + d, n)
            return device(z, y, coord, c), coord
        coord = lax.rem(y + d, n)
        return device(z, coord, x, c), coord

    def plane_peer(p, e):
        d0, d1 = e // n, e % n
        if p == 0:
            yy, zz = lax.rem(y + d0, n), lax.rem(z + d1, n)
            return device(zz, yy, x, c), yy * n + zz
        zz, xx = lax.rem(z + d0, n), lax.rem(x + d1, n)
        return device(zz, y, xx, c), zz * n + xx

    def remote(src, dst, r, s, dev):
        return pltpu.make_async_remote_copy(src_ref=src, dst_ref=dst, send_sem=send_sem.at[r, s], recv_sem=recv_sem.at[r, s],
                                            device_id=(dev,), device_id_type=MESH)

    def own_q(p):
        return c * half + p * quarter + ring_at[p]

    def strip_of(m):
        return pl.ds(pl.multiple_of(m * strip, 8), strip)

    def core_scatter(r, p):
        return remote(acc.at[r, pl.ds((1 - c) * half + p * quarter, quarter)], rc.at[r, p], r, p, sibling)

    def ring_scatter(r, p):
        out = []
        for d in range(1, n):
            dev, coord = ring_peer(p, d)
            out.append(remote(acc.at[r, c * half + p * quarter + coord], rr.at[r, p, d - 1], r, 2 + 3 * p + d - 1, dev))
        return out

    def plane_scatter(r, p):
        out = []
        for e in range(1, plane):
            dev, m = plane_peer(p, e)
            out.append(remote(acc.at[r, own_q(p), strip_of(m)], rp.at[r, p, e - 1], r, 8 + p, dev))
        return out

    def plane_gather(r, p):
        out = []
        for e in range(1, plane):
            dev, _ = plane_peer(p, e)
            block = wbuf.at[r, own_q(p), strip_of(plane_at[p])]
            out.append(remote(block, block, r, 10 + p, dev))
        return out

    def plane_total(r, s, p):
        return remote(rp.at[r, p], rp.at[r, p], r, s + p, sibling)

    def ring_gather(r, p):
        out = []
        for d in range(1, n):
            dev, _ = ring_peer(p, d)
            block = wbuf.at[r, own_q(p)]
            out.append(remote(block, block, r, 12 + 3 * p + d - 1, dev))
        return out

    def core_gather(r, q):
        block = wbuf.at[r, q]
        return remote(block, block, r, 18, sibling)

    def core_total(r):
        block = wbuf.at[r, pl.ds(c * half, half)]
        return remote(block, block, r, 18, sibling)

    barrier = pltpu.get_barrier_semaphore()
    peers = [sibling] + [plane_peer(0, e)[0] for e in range(1, plane)]
    peers += [plane_peer(1, e)[0] for e in range(1, plane) if e % n]
    for dev in peers:
        pl.semaphore_signal(barrier, inc=1, device_id=(dev,), device_id_type=MESH)
    pl.semaphore_wait(barrier, len(peers))

    big = pairs * 16
    spread = jnp.where(lax.broadcasted_iota(jnp.int32, (big, pairs), 0) // 16
                       == lax.broadcasted_iota(jnp.int32, (big, pairs), 1), 1.0, 0.0).astype(BF16)
    spread_t = jnp.where(lax.broadcasted_iota(jnp.int32, (pairs, big), 1) // 16
                         == lax.broadcasted_iota(jnp.int32, (pairs, big), 0), 1.0, 0.0).astype(BF16)
    diagonal = (lax.rem(lax.broadcasted_iota(jnp.int32, (big, big), 0), 16)
                == lax.rem(lax.broadcasted_iota(jnp.int32, (big, big), 1), 16))

    def expand(i, carry):
        talls = [jnp.dot(spread, phys_ref[4 * i + k], preferred_element_type=F32).astype(BF16) for k in range(4)]
        for k in range(4):
            full = jnp.dot(talls[k], spread_t, preferred_element_type=F32)
            wide[4 * i + k] = jnp.where(diagonal, full, 0.0).astype(BF16)
        return carry

    lax.fori_loop(0, terms // 4, expand, 0)

    chunk = 2 * bond
    chunks = rows // chunk

    def rows_of(i):
        return pl.ds(pl.multiple_of(i * chunk, 8), chunk)

    def fold(t):
        return jnp.sum(t.reshape(chunk // 8, 8, bond), axis=0)

    def total(t):
        return jnp.sum(t, axis=(0, 1), keepdims=True)

    zero_tile = jnp.zeros((8, bond), F32)

    def put_vector(r, nxt, i, part):
        v[r, nxt, rows_of(i), :] = part
        small = part.astype(BF16)
        for h in range(2):
            for g in range(bond // 16):
                u[r, g, 2 * i + h] = small[h * bond + g * 16:h * bond + (g + 1) * 16]

    def put_row(r, nxt, j):
        vec_ref[r, j] = v[r, nxt, pl.ds(me, pairs, stride=bond), :]

    def first_vector(r, carry):
        def norm_body(i, s):
            part = psi_ref[r, rows_of(i), :]
            return s + fold(part * part)

        norm = jnp.sqrt(total(lax.fori_loop(0, chunks, norm_body, zero_tile)) / n_elems)

        def scale_body(i, s):
            cols = [psi_ref[r, pl.ds(2 * i + h, bond, stride=pairs), :] for h in range(2)]
            put_vector(r, 0, i, jnp.concatenate(cols, axis=0) / norm)
            v[r, 1, rows_of(i), :] = jnp.zeros((chunk, bond), F32)
            return s

        lax.fori_loop(0, chunks, scale_body, 0)
        beta_prev[r] = zero_tile
        put_row(r, 0, 0)
        return carry

    lax.fori_loop(0, roots, first_vector, 0)

    def update(r, j):
        cur, nxt = lax.rem(j, 2), lax.rem(j + 1, 2)

        def sigma(i):
            return wbuf[r, pl.ds(2 * i, 2)].reshape(chunk, bond)

        def alpha_body(i, s):
            return s + fold(sigma(i) * v[r, cur, rows_of(i), :])

        alpha = total(lax.fori_loop(0, chunks, alpha_body, zero_tile, unroll=2)) / n_elems
        before = beta_prev[r][0:1, 0:1]

        def residual_body(i, s):
            res = sigma(i) - alpha * v[r, cur, rows_of(i), :] - before * v[r, nxt, rows_of(i), :]
            wbuf[r, pl.ds(2 * i, 2)] = res.reshape(2, bond, bond)
            return s + fold(res * res)

        beta = jnp.sqrt(total(lax.fori_loop(0, chunks, residual_body, zero_tile, unroll=2)) / n_elems)

        def next_body(i, s):
            put_vector(r, nxt, i, sigma(i) / beta)
            return s

        lax.fori_loop(0, chunks, next_body, 0)
        alpha_ref[r, j] = jnp.broadcast_to(alpha, (8, bond))
        beta_ref[r, j] = jnp.broadcast_to(beta, (8, bond))
        beta_prev[r] = jnp.broadcast_to(beta, (8, bond))
        put_row(r, nxt, j + 1)

    def right_mid(r, first):
        units = [(pp, g2) for pp in range(PAIRS_PER_ITER) for g2 in range(bond // 32)]
        weights = [jnp.concatenate([right_ref[2 * (first + pp)], right_ref[2 * (first + pp) + 1]], axis=1)
                   for pp in range(PAIRS_PER_ITER)]

        def right(unit):
            pp, g2 = unit
            return [jnp.dot(u[r, g].reshape(big, bond), weights[pp], preferred_element_type=F32).astype(BF16)
                    for g in (2 * g2, 2 * g2 + 1)]

        def mid(unit, ys):
            pp, g2 = unit
            for k in range(2):
                rhs = jnp.concatenate([t[:, k * bond:(k + 1) * bond] for t in ys], axis=1)
                term = 2 * (first + pp) + k
                out = jnp.dot(wide[term], rhs, preferred_element_type=F32).astype(BF16)
                for h in range(2):
                    g = 2 * g2 + h
                    zbuf[term, :, g * 16:(g + 1) * 16, :] = out[:, h * bond:(h + 1) * bond].reshape(pairs, 16, bond)

        ys = right(units[0])
        for i, unit in enumerate(units):
            after = right(units[i + 1]) if i + 1 < len(units) else None
            mid(unit, ys)
            ys = after

    def left(r, q0):
        lhs = jnp.concatenate([left_ref[k] for k in range(terms)], axis=1)
        for qp in range(quarter // 2):
            q = q0 + 2 * qp
            cols = [jnp.concatenate([zbuf[k, q + h] for k in range(terms)], axis=0) for h in range(2)]
            out = jnp.dot(lhs, jnp.concatenate(cols, axis=1), preferred_element_type=F32)
            for h in range(2):
                acc[r, q + h] = out[:, h * bond:(h + 1) * bond]

    def start_ring(r, p):
        core_scatter(r, p).wait()
        for i in range(quarter):
            q = c * half + p * quarter + i
            acc[r, q] = acc[r, q] + rc[r, p, i]
        for copy in ring_scatter(r, p):
            copy.start()

    def ring_to_plane(r):
        for p in range(2):
            for copy in ring_scatter(r, p):
                copy.wait()
            acc[r, own_q(p)] = acc[r, own_q(p)] + rr[r, p, 0] + rr[r, p, 1] + rr[r, p, 2]
            for copy in plane_scatter(r, p):
                copy.start()

    def plane_to_gather(r):
        for p in range(2):
            done = plane_total(r, 8, p)
            done.wait_send()
            done.wait_recv()
            at = strip_of(plane_at[p])
            sums = [acc[r, own_q(p), at, :]] + [rp[r, p, e] for e in range(plane - 1)]
            while len(sums) > 1:
                sums = [a + b for a, b in zip(sums[::2], sums[1::2])]
            wbuf[r, own_q(p), at, :] = sums[0]
            for copy in plane_gather(r, p):
                copy.start()

    def plane_to_ring(r):
        for p in range(2):
            done = plane_total(r, 10, p)
            done.wait_send()
            done.wait_recv()
            for copy in ring_gather(r, p):
                copy.start()
            core_gather(r, own_q(p)).start()

    def finish_gather(r):
        for d in (1, 3, 2):
            for p in range(2):
                copy = ring_gather(r, p)[d - 1]
                copy.wait_send()
                copy.wait_recv()
                back = lax.rem(ring_at[p] + n - d, n)
                core_gather(r, c * half + p * quarter + back).start()
        done = core_total(r)
        done.wait_send()
        done.wait_recv()

    slots = roots * steps

    def slot(s, carry):
        r = lax.rem(s, roots)
        r1 = lax.rem(s + roots - 1, roots)
        r2 = lax.rem(s + roots - 2, roots)
        computing = s < slots
        scattering = jnp.logical_and(s >= 1, s < slots + 1)
        gathering = s >= 2

        def step(i, t):
            @pl.when(jnp.logical_and(gathering, i == GATHER_HOOK))
            def _():
                plane_to_ring(r2)

            @pl.when(jnp.logical_and(scattering, i == SCATTER_HOOK))
            def _():
                ring_to_plane(r1)

            @pl.when(computing)
            def _():
                right_mid(r, i * PAIRS_PER_ITER)
            return t

        lax.fori_loop(0, terms // 2 // PAIRS_PER_ITER, step, 0)

        @pl.when(computing)
        def _():
            for p in range(2):
                left(r, (1 - c) * half + p * quarter)
                core_scatter(r, p).start()
            for p in range(2):
                left(r, c * half + p * quarter)
                start_ring(r, p)

        @pl.when(scattering)
        def _():
            plane_to_gather(r1)

        @pl.when(gathering)
        def _():
            finish_gather(r2)
            update(r2, (s - 2) // roots)
        return carry

    lax.fori_loop(0, slots + 2, slot, 0)


def build(n, steps, roots, bond, pairs, terms):
    rows = pairs * bond
    half, quarter, plane = pairs // 2, pairs // 4, n * n
    vm = pl.BlockSpec(memory_space=pltpu.VMEM)
    return pl.pallas_call(
        functools.partial(lanczos_kernel, n, steps),
        out_shape=(jax.ShapeDtypeStruct((roots, steps + 1, pairs, bond), F32),
                   jax.ShapeDtypeStruct((roots, steps, 8, bond), F32),
                   jax.ShapeDtypeStruct((roots, steps, 8, bond), F32)),
        in_specs=[vm] * 4,
        out_specs=(vm, vm, vm),
        scratch_shapes=[
            pltpu.VMEM((roots, 2, rows, bond), F32),
            pltpu.VMEM((roots, bond // 16, pairs, 16, bond), BF16),
            pltpu.VMEM((terms, pairs * 16, pairs * 16), BF16),
            pltpu.VMEM((terms, pairs, bond, bond), BF16),
            pltpu.VMEM((roots, pairs, bond, bond), F32),
            pltpu.VMEM((roots, pairs, bond, bond), F32),
            pltpu.VMEM((roots, 2, quarter, bond, bond), F32),
            pltpu.VMEM((roots, 2, n - 1, bond, bond), F32),
            pltpu.VMEM((roots, 2, plane - 1, bond // plane, bond), F32),
            pltpu.VMEM((roots, 8, bond), F32),
            pltpu.SemaphoreType.DMA((roots, SEMS)),
            pltpu.SemaphoreType.DMA((roots, SEMS)),
        ],
        compiler_params=pltpu.CompilerParams(collective_id=0, has_side_effects=True,
                                             vmem_limit_bytes=60 * 1024 * 1024),
        name='lanczos',
    )


def solution(mesh):
    def device_fn(psi, left_loc, phys_loc, right_loc):
        roots, bond, phys = psi.shape[0], psi.shape[1], psi.shape[2]
        pairs = phys * phys
        vecs, alpha, beta = build(4, LANCZOS_STEPS, roots, bond, pairs, left_loc.shape[0])(
            psi.reshape(roots, bond * pairs, bond), left_loc, phys_loc, right_loc)
        return (vecs.reshape(roots, LANCZOS_STEPS + 1, 1, phys, phys, bond), alpha[:, :, 0, 0], beta[:, :, 0, 0])

    return jax.shard_map(device_fn, mesh=mesh, in_specs=(P(), P('terms'), P('terms'), P('terms')),
                         out_specs=(P(None, None, 'terms'), P(), P()), check_vma=False)
```

time: 2890 us -> 297 us (0.10)
  waiting for transfers between devices: 1550 us -> 0 us
  blocking collectives: 762 us -> 0 us
  matrix products: 500 us -> 0 us
  Pallas kernels: 0 us -> 291 us
    reduce_scatter x6 -> x0, waiting for transfers between devices: 1240 us -> none  [device_fn(): lax.psum_scatter(part_sigma, 'terms', scatter_dimension=1, tiled=True)]
    psum x12 -> x0, blocking collectives: 762 us -> none  [the longest x6 388 us: device_fn(): alpha = lax.psum(jnp.sum(sigma * v_cur, axis=(1, 2, 3)), 'terms') / n_elems]
    dot_general x18 -> x0, matrix products: 500 us -> none  [the longest x6 213 us: device_fn(): jnp.einsum('kqu,krcub->krcqb', phys_loc, right_part, preferred_element_ty...]
    all_gather x5 -> x0, waiting for transfers between devices: 308 us -> none  [device_fn(): lax.all_gather(v_next.astype(jnp.bfloat16), 'terms', axis=1, tiled=True)]
    pallas_call x0 -> x1, Pallas kernels: none -> 291 us  [device_fn(): build(4, LANCZOS_STEPS, roots, bond, pairs, left_loc.shape[0])]
  transfers between devices with their start and end apart: 11 -> 0, of which waited for: 11 -> 0; matrix products, arithmetic and copies ran while one was open for 0% -> 0% of each run, Pallas kernels for 0% -> 0%
where the time goes in v2:
time: 297 us
  Pallas kernels  291 us (98%)
  local copies, waits for them, and re-layouts  4.85 us (2%)
    pallas_call x1, Pallas kernels, device_fn(): build(4, LANCZOS_STEPS, roots, bond, pairs, left_loc.shape[0])  291 us

profile of v2, /device:TPU:1, one launch (start us, length us, event | category | flops | bytes accessed | tf_op | source)
XLA Modules:
  0.0 296.8 jit_solution(17804399110469485463)
XLA Ops:
  0.6 1.6 copy.9.phys_ref
  2.2 291.3 %lanczos.1 = (f32[3,7,16,128]{3,2,1,0:T(8,128)}, f32[3,6,8,128]{3,2,1,0:T(8,128)}, f32[3,6,8,128]{3,2,1,0:T(8,128)}) custom-call(f32[3,2048,128]{2,1,0:T(8,128)} %bitcast.4, bf16[24,128,128]{2,1,0:T(8,128)(2,1)} %left_ref.1, bf16[24,16,16]{2,1,0:T(8,128)(2,1)} %copy.9.phys_ref, bf16[24,128,128]{2,1,0:T(8,128)(2,1)} %right_ref.1), custom_call_target="tpu_custom_call" | custom-call | tf_op jit(solution)/shard_map/lanczos/pallas_call | solution.py:379
  293.6 1.6 slice_reduce_fusion
  295.2 1.6 copy.12

commit v3 on v2

--- a/solution.py
+++ b/solution.py
@@ -12,8 +12,7 @@
 F32 = jnp.float32
 BF16 = jnp.bfloat16
 PAIRS_PER_ITER = 3
-SCATTER_HOOK = 3
-GATHER_HOOK = 2
+RING_SCATTER_AT, PLANE_SCATTER_AT, PLANE_GATHER_AT, RING_GATHER_AT = 2, 7, 2, 7
 SEMS = 19
 
 
@@ -77,16 +76,18 @@
             out.append(remote(acc.at[r, c * half + p * quarter + coord], rr.at[r, p, d - 1], r, 2 + 3 * p + d - 1, dev))
         return out
 
+    order = sorted(range(1, plane), key=lambda e: -min(e // n, n - e // n) - min(e % n, n - e % n))
+
     def plane_scatter(r, p):
         out = []
-        for e in range(1, plane):
+        for e in order:
             dev, m = plane_peer(p, e)
             out.append(remote(acc.at[r, own_q(p), strip_of(m)], rp.at[r, p, e - 1], r, 8 + p, dev))
         return out
 
     def plane_gather(r, p):
         out = []
-        for e in range(1, plane):
+        for e in order:
             dev, _ = plane_peer(p, e)
             block = wbuf.at[r, own_q(p), strip_of(plane_at[p])]
             out.append(remote(block, block, r, 10 + p, dev))
@@ -116,7 +117,6 @@
     peers += [plane_peer(1, e)[0] for e in range(1, plane) if e % n]
     for dev in peers:
         pl.semaphore_signal(barrier, inc=1, device_id=(dev,), device_id_type=MESH)
-    pl.semaphore_wait(barrier, len(peers))
 
     big = pairs * 16
     spread = jnp.where(lax.broadcasted_iota(jnp.int32, (big, pairs), 0) // 16
@@ -178,6 +178,7 @@
         return carry
 
     lax.fori_loop(0, roots, first_vector, 0)
+    pl.semaphore_wait(barrier, len(peers))
 
     def update(r, j):
         cur, nxt = lax.rem(j, 2), lax.rem(j + 1, 2)
@@ -203,8 +204,8 @@
             return s
 
         lax.fori_loop(0, chunks, next_body, 0)
-        alpha_ref[r, j] = jnp.broadcast_to(alpha, (8, bond))
-        beta_ref[r, j] = jnp.broadcast_to(beta, (8, bond))
+        alpha_ref[r, j] = alpha[0, 0]
+        beta_ref[r, j] = beta[0, 0]
         beta_prev[r] = jnp.broadcast_to(beta, (8, bond))
         put_row(r, nxt, j + 1)
 
@@ -243,13 +244,16 @@
             for h in range(2):
                 acc[r, q + h] = out[:, h * bond:(h + 1) * bond]
 
-    def start_ring(r, p):
-        core_scatter(r, p).wait()
-        for i in range(quarter):
-            q = c * half + p * quarter + i
-            acc[r, q] = acc[r, q] + rc[r, p, i]
-        for copy in ring_scatter(r, p):
-            copy.start()
+    def start_ring(r):
+        for p in range(2):
+            core_scatter(r, p).wait()
+            for i in range(quarter):
+                q = c * half + p * quarter + i
+                acc[r, q] = acc[r, q] + rc[r, p, i]
+        both = [ring_scatter(r, p) for p in range(2)]
+        for d in (2, 1, 3):
+            for p in range(2):
+                both[p][d - 1].start()
 
     def ring_to_plane(r):
         for p in range(2):
@@ -277,11 +281,14 @@
             done = plane_total(r, 10, p)
             done.wait_send()
             done.wait_recv()
-            for copy in ring_gather(r, p):
-                copy.start()
+        both = [ring_gather(r, p) for p in range(2)]
+        for d in (2, 1, 3):
+            for p in range(2):
+                both[p][d - 1].start()
+        for p in range(2):
             core_gather(r, own_q(p)).start()
 
-    def finish_gather(r):
+    def ring_to_core(r):
         for d in (1, 3, 2):
             for p in range(2):
                 copy = ring_gather(r, p)[d - 1]
@@ -289,10 +296,14 @@
                 copy.wait_recv()
                 back = lax.rem(ring_at[p] + n - d, n)
                 core_gather(r, c * half + p * quarter + back).start()
+
+    def finish_gather(r):
         done = core_total(r)
         done.wait_send()
         done.wait_recv()
 
+    RM_STEPS = terms // 2 // PAIRS_PER_ITER
+    PLACES = (RING_SCATTER_AT, PLANE_SCATTER_AT, PLANE_GATHER_AT, RING_GATHER_AT)
     slots = roots * steps
 
     def slot(s, carry):
@@ -303,34 +314,43 @@
         scattering = jnp.logical_and(s >= 1, s < slots + 1)
         gathering = s >= 2
 
+        def hooks(at, here):
+            for place, guard, root, work in ((RING_SCATTER_AT, scattering, r1, ring_to_plane),
+                                             (PLANE_GATHER_AT, gathering, r2, plane_to_ring),
+                                             (PLANE_SCATTER_AT, scattering, r1, plane_to_gather),
+                                             (RING_GATHER_AT, gathering, r2, ring_to_core)):
+                if place in here:
+                    pl.when(jnp.logical_and(guard, at == place))(functools.partial(work, root))
+
         def step(i, t):
-            @pl.when(jnp.logical_and(gathering, i == GATHER_HOOK))
-            def _():
-                plane_to_ring(r2)
-
-            @pl.when(jnp.logical_and(scattering, i == SCATTER_HOOK))
-            def _():
-                ring_to_plane(r1)
+            hooks(i, range(RM_STEPS))
 
             @pl.when(computing)
             def _():
                 right_mid(r, i * PAIRS_PER_ITER)
             return t
 
-        lax.fori_loop(0, terms // 2 // PAIRS_PER_ITER, step, 0)
-
-        @pl.when(computing)
-        def _():
-            for p in range(2):
+        lax.fori_loop(0, RM_STEPS, step, 0)
+
+        def left_part(k):
+            p = k % 2
+            if k < 2:
                 left(r, (1 - c) * half + p * quarter)
                 core_scatter(r, p).start()
-            for p in range(2):
+            else:
                 left(r, c * half + p * quarter)
-                start_ring(r, p)
-
-        @pl.when(scattering)
-        def _():
-            plane_to_gather(r1)
+                if k == 3:
+                    start_ring(r)
+
+        group = []
+        for k in range(4):
+            if RM_STEPS + k in PLACES and group:
+                pl.when(computing)(functools.partial(lambda ks: [left_part(m) for m in ks] and None, group))
+                group = []
+            hooks(RM_STEPS + k, (RM_STEPS + k,))
+            group.append(k)
+        pl.when(computing)(functools.partial(lambda ks: [left_part(m) for m in ks] and None, group))
+        hooks(RM_STEPS + 4, (RM_STEPS + 4,))
 
         @pl.when(gathering)
         def _():
@@ -348,10 +368,9 @@
     return pl.pallas_call(
         functools.partial(lanczos_kernel, n, steps),
         out_shape=(jax.ShapeDtypeStruct((roots, steps + 1, pairs, bond), F32),
-                   jax.ShapeDtypeStruct((roots, steps, 8, bond), F32),
-                   jax.ShapeDtypeStruct((roots, steps, 8, bond), F32)),
+                   jax.ShapeDtypeStruct((roots, steps), F32), jax.ShapeDtypeStruct((roots, steps), F32)),
         in_specs=[vm] * 4,
-        out_specs=(vm, vm, vm),
+        out_specs=(vm, pl.BlockSpec(memory_space=pltpu.SMEM), pl.BlockSpec(memory_space=pltpu.SMEM)),
         scratch_shapes=[
             pltpu.VMEM((roots, 2, rows, bond), F32),
             pltpu.VMEM((roots, bond // 16, pairs, 16, bond), BF16),
@@ -378,7 +397,7 @@
         pairs = phys * phys
         vecs, alpha, beta = build(4, LANCZOS_STEPS, roots, bond, pairs, left_loc.shape[0])(
             psi.reshape(roots, bond * pairs, bond), left_loc, phys_loc, right_loc)
-        return (vecs.reshape(roots, LANCZOS_STEPS + 1, 1, phys, phys, bond), alpha[:, :, 0, 0], beta[:, :, 0, 0])
+        return (vecs.reshape(roots, LANCZOS_STEPS + 1, 1, phys, phys, bond), alpha, beta)
 
     return jax.shard_map(device_fn, mesh=mesh, in_specs=(P(), P('terms'), P('terms'), P('terms')),
                          out_specs=(P(None, None, 'terms'), P(), P()), check_vma=False)

time: 297 us -> 268 us (0.902)
  Pallas kernels: 291 us -> 261 us
    pallas_call x1, Pallas kernels: 291 us -> 261 us  [device_fn(): build(4, LANCZOS_STEPS, roots, bond, pairs, left_loc.shape[0])]
where the time goes in v3:
time: 268 us
  Pallas kernels  261 us (97%)
  local copies, waits for them, and re-layouts  5.68 us (2%)
    pallas_call x1, Pallas kernels, device_fn(): build(4, LANCZOS_STEPS, roots, bond, pairs, left_loc.shape[0])  261 us
    unnamed x4, local copies, waits for them, and re-layouts  5.68 us

profile of v3, /device:TPU:1, one launch (start us, length us, event | category | flops | bytes accessed | tf_op | source)
XLA Modules:
  0.0 267.6 jit_solution(9792652389458900289)
XLA Ops:
  0.6 1.6 copy.7.phys_ref
  2.2 261.3 %lanczos.1 = (f32[3,7,16,128]{3,2,1,0:T(8,128)}, f32[3,6]{1,0:T(4,128)}, f32[3,6]{1,0:T(4,128)}) custom-call(f32[3,2048,128]{2,1,0:T(8,128)} %bitcast.4, bf16[24,128,128]{2,1,0:T(8,128)(2,1)} %left_ref.1, bf16[24,16,16]{2,1,0:T(8,128)(2,1)} %copy.7.phys_ref, bf16[24,128,128]{2,1,0:T(8,128)(2,1)} %right_ref.1), custom_call_target="tpu_custom_call" | custom-call | tf_op jit(solution)/shard_map/lanczos/pallas_call | solution.py:398
  263.5 1.6 copy.12
  265.1 1.2 copy.13
  266.4 1.2 copy.14

commit v4 on v3

--- a/solution.py
+++ b/solution.py
@@ -189,7 +189,13 @@
         def alpha_body(i, s):
             return s + fold(sigma(i) * v[r, cur, rows_of(i), :])
 
-        alpha = total(lax.fori_loop(0, chunks, alpha_body, zero_tile, unroll=2)) / n_elems
+        def alpha_half(which):
+            first = which * (chunks // 2)
+            return lax.fori_loop(0, chunks // 2, lambda i, s: alpha_body(first + i, s), zero_tile)
+
+        mine = alpha_half(c)
+        finish_gather(r)
+        alpha = total(mine + alpha_half(1 - c)) / n_elems
         before = beta_prev[r][0:1, 0:1]
 
         def residual_body(i, s):
@@ -203,7 +209,7 @@
             put_vector(r, nxt, i, sigma(i) / beta)
             return s
 
-        lax.fori_loop(0, chunks, next_body, 0)
+        lax.fori_loop(0, chunks, next_body, 0, unroll=2)
         alpha_ref[r, j] = alpha[0, 0]
         beta_ref[r, j] = beta[0, 0]
         beta_prev[r] = jnp.broadcast_to(beta, (8, bond))
@@ -260,7 +266,8 @@
             for copy in ring_scatter(r, p):
                 copy.wait()
             acc[r, own_q(p)] = acc[r, own_q(p)] + rr[r, p, 0] + rr[r, p, 1] + rr[r, p, 2]
-            for copy in plane_scatter(r, p):
+        for pair in zip(plane_scatter(r, 0), plane_scatter(r, 1)):
+            for copy in pair:
                 copy.start()
 
     def plane_to_gather(r):
@@ -273,7 +280,8 @@
             while len(sums) > 1:
                 sums = [a + b for a, b in zip(sums[::2], sums[1::2])]
             wbuf[r, own_q(p), at, :] = sums[0]
-            for copy in plane_gather(r, p):
+        for pair in zip(plane_gather(r, 0), plane_gather(r, 1)):
+            for copy in pair:
                 copy.start()
 
     def plane_to_ring(r):
@@ -354,7 +362,6 @@
 
         @pl.when(gathering)
         def _():
-            finish_gather(r2)
             update(r2, (s - 2) // roots)
         return carry
 

time: 268 us -> 266 us (level)
  no operation moved by 1% of the time
where the time goes in v4:
time: 266 us
  Pallas kernels  260 us (98%)
  local copies, waits for them, and re-layouts  5.68 us (2%)
    pallas_call x1, Pallas kernels, device_fn(): build(4, LANCZOS_STEPS, roots, bond, pairs, left_loc.shape[0])  260 us
    unnamed x4, local copies, waits for them, and re-layouts  5.68 us

profile of v4, /device:TPU:1, one launch (start us, length us, event | category | flops | bytes accessed | tf_op | source)
XLA Modules:
  0.0 266.0 jit_solution(8197059781781690458)
XLA Ops:
  0.6 1.6 copy.7.phys_ref
  2.2 259.7 %lanczos.1 = (f32[3,7,16,128]{3,2,1,0:T(8,128)}, f32[3,6]{1,0:T(4,128)}, f32[3,6]{1,0:T(4,128)}) custom-call(f32[3,2048,128]{2,1,0:T(8,128)} %bitcast.4, bf16[24,128,128]{2,1,0:T(8,128)(2,1)} %left_ref.1, bf16[24,16,16]{2,1,0:T(8,128)(2,1)} %copy.7.phys_ref, bf16[24,128,128]{2,1,0:T(8,128)(2,1)} %right_ref.1), custom_call_target="tpu_custom_call" | custom-call | tf_op jit(solution)/shard_map/lanczos/pallas_call | solution.py:405
  261.9 1.6 copy.12
  263.5 1.2 copy.13
  264.8 1.2 copy.14
